TPU v7x, 32 devices: a whole 2x2x4 slice. The times are simulated.
32 devices in a mesh: row: 8 (over z, x), col: 4 (over y, core).
Axes of the slice: x: 2, y: 2, z: 4, core: 2. Of those that a mesh axis runs over, the one named last changes fastest.
Arguments:
- hub_seeds: bfloat16 [192, 64, 128], P('row'), may hold values from -6 to 6
- tile_blocks: bfloat16 [8192, 128, 128], P(('row', 'col')), may hold values from -8 to 8
- tile_rows: int32 [8192], P(('row', 'col')), may hold values from 0 to 127, as said below
- tile_cols: int32 [8192], P(('row', 'col')), may hold values from 0 to 127, as said below
- tile_count: int32 [32], P(('row', 'col')), may hold values from 64 to 256, as said below
- row_blocks: int32 [8], replicated, may hold values from 8 to 24, as said below
Outputs:
- authority: bfloat16 [128, 64, 128], P(('row', 'col'))
- hub_scores: bfloat16 [192, 64, 128], P('row')
Inputs may be any that keep to these rules, and one draw needn't show every extreme that they name: Row range r covers row blocks starts[r] to starts[r] + row_blocks[r] - 1, the ranges in order and together all 128 blocks; the longest range has exactly 24 blocks in every draw. `tile_rows`: every tile of a device lies in the row range of the device's row index; no pair of row block and column block repeats within a device. `tile_cols`: A device with column index c holds only column blocks b with (b // 4) % 4 == c. The live tiles of a device are its first tile_count slots; some device has all 256 slots live in every draw.
All inputs are finite; a program needn't handle non-finite values.
Results may differ from a plain program's by a relative error of at most 0.02.
Values may be sent and summed in bfloat16 or wider, within the bound.
A program may use at most 192 MiB of HBM per device.

v0:
```python
import jax
import jax.numpy as jnp
from jax import lax
from jax.sharding import PartitionSpec as P

ITERS = 2
RB_DEV = 16


def local(hub_seeds, tile_blocks, tile_rows, tile_cols, tile_count, row_blocks):
    own_row = lax.axis_index("row")
    row_devs = lax.axis_size("row")
    col_devs = lax.axis_size("col")
    slot_count = hub_seeds.shape[0]
    tile_side = tile_blocks.shape[1]
    tile_slots = tile_blocks.shape[0]
    group_len = RB_DEV // col_devs
    set_blocks = group_len * row_devs
    host_count = RB_DEV * row_devs * tile_side
    span_length = row_blocks[own_row]
    before = jnp.arange(row_devs, dtype=jnp.int32) < own_row
    first_block = jnp.sum(jnp.where(before, row_blocks, 0))
    live_tile = jnp.arange(tile_slots, dtype=jnp.int32) < tile_count[0]
    row_slot = jnp.where(live_tile, tile_rows - first_block, slot_count)
    col_slot = jnp.where(
        live_tile,
        tile_cols // group_len // col_devs * group_len + tile_cols % group_len,
        set_blocks,
    )
    row_pick = jnp.clip(row_slot, 0, slot_count - 1)
    col_pick = jnp.clip(col_slot, 0, set_blocks - 1)
    usable = jnp.arange(slot_count, dtype=jnp.int32) < span_length
    hub_now = jnp.where(usable[:, None, None], hub_seeds, jnp.zeros_like(hub_seeds))
    authority = None
    for iteration in range(ITERS):
        picked = jnp.take(hub_now, row_pick, axis=0, mode="clip")
        products = jnp.einsum(
            "tkr,trc->tkc", picked, tile_blocks, preferred_element_type=jnp.float32
        )
        set_terms = jax.ops.segment_sum(products, col_slot, num_segments=set_blocks, mode="drop")
        raw_set = lax.psum(set_terms.astype(jnp.bfloat16), "row").astype(jnp.float32)
        squares = lax.psum(jnp.sum(raw_set * raw_set, axis=(0, 2)), "col")
        factor = 1.0 / jnp.sqrt(squares / host_count + 1.0)
        column_set = (raw_set * factor[None, :, None]).astype(jnp.bfloat16)
        authority = lax.dynamic_slice_in_dim(column_set, own_row * group_len, group_len, 0)
        picked_cols = jnp.take(column_set, col_pick, axis=0, mode="clip")
        back_products = jnp.einsum(
            "tkc,trc->tkr", picked_cols, tile_blocks, preferred_element_type=jnp.float32
        )
        hub_terms = jax.ops.segment_sum(
            back_products, row_slot, num_segments=slot_count, mode="drop"
        )
        raw_hub = lax.psum(hub_terms.astype(jnp.bfloat16), "col").astype(jnp.float32)
        squares = lax.psum(jnp.sum(raw_hub * raw_hub, axis=(0, 2)), "row")
        factor = 1.0 / jnp.sqrt(squares / host_count + 1.0)
        hub_now = (raw_hub * factor[None, :, None]).astype(jnp.bfloat16)
    return (authority, hub_now)


def solution(mesh):
    return jax.shard_map(
        local,
        mesh=mesh,
        in_specs=(
            P("row", None, None),
            P(("row", "col"), None, None),
            P(("row", "col")),
            P(("row", "col")),
            P(("row", "col")),
            P(),
        ),
        out_specs=(P(("row", "col"), None, None), P("row", None, None)),
        check_vma=False,
    )
```

profile of v0, /device:TPU:0, one launch (start us, length us, event | category | flops | bytes accessed | tf_op | source)
XLA Modules:
  0.0 463.2 jit_solution(11632191388393047059)
XLA Ops:
  7.2 0.0 all-reduce.5.cloned.1.call-start
  7.2 1.3 fusion.10
  8.5 1.2 dynamic_slice.6
  9.7 0.6 iota_compare_fusion.1
  11.0 1.4 broadcast_clamp_fusion
  12.4 1.1 broadcast_select_fusion
  13.5 3.1 gather_fusion
  16.6 10.2 %fusion.12 = f32[256,64,128]{2,1,0:T(8,128)} fusion(bf16[256,64,128]{2,1,0:T(8,128)(2,1)} %gather_fusion, bf16[256,128,128]{2,1,0:T(8,128)(2,1)} %param.7), kind=kOutput, calls=%fused_computation.50 | convolution fusion | flops 536870912 | bytes 20971520 | tf_op jit(solution)/shard_map/tkr,trc->tkc/dot_general | solution.py:37
  26.8 0.1 broadcast.40.clone
  26.9 26.3 %scatter_fusion = f32[32,64,128]{2,1,0:T(8,128)S(1)} fusion(f32[32,64,128]{2,1,0:T(8,128)S(1)} %broadcast.40.clone, s32[256]{0:T(256)S(1)} %get-tuple-element.3, f32[256,64,128]{2,1,0:T(8,128)} %fusion.12), kind=kCustom, calls=%fused_computation.4 | custom fusion | flops 2097152 | bytes 25166848 | tf_op jit(solution)/shard_map/scatter-add | solution.py:40
  53.2 0.9 convert_element_type.36
  54.1 0.0 all-reduce.5.cloned.1.call-update
  54.2 0.0 all-reduce.7.cloned.1.call-start
  54.2 75.3 %all-reduce.5.cloned.1.call-done = bf16[32,64,128]{2,1,0:T(8,128)(2,1)} async-done(((bf16[32,64,128]{2,1,0:T(8,128)(2,1)}), bf16[32,64,128]{2,1,0:T(8,128)(2,1)}) %all-reduce.5.cloned.1.call-update) | async-done | bytes 524304 | tf_op jit(solution)/shard_map/psum | solution.py:41
  129.5 1.3 fusion
  130.8 5.7 %psum.57 = f32[64]{0:T(128)S(1)} all-reduce(f32[64]{0:T(128)S(1)} %fusion), channel_id=1, replica_groups=mesh['row'=8,'col'=4] {'col'}, use_global_device_ids=true, to_apply=%region_4.5 | all-reduce | flops 64 | bytes 512 | tf_op jit(solution)/shard_map/psum | solution.py:42
  136.5 1.3 fusion.1
  137.7 3.1 gather_fusion.1
  140.8 13.7 %fusion.13 = f32[256,64,128]{2,1,0:T(8,128)} fusion(bf16[256,64,128]{2,1,0:T(8,128)(2,1)} %gather_fusion.1, bf16[256,128,128]{2,1,0:T(8,128)(2,1)} %param.7), kind=kOutput, calls=%fused_computation.51 | convolution fusion | flops 536870912 | bytes 20971520 | tf_op jit(solution)/shard_map/tkc,trc->tkr/dot_general | solution.py:47
  154.5 0.1 broadcast.42.clone
  154.6 26.3 %scatter_fusion.1 = f32[24,64,128]{2,1,0:T(8,128)S(1)} fusion(f32[24,64,128]{2,1,0:T(8,128)S(1)} %broadcast.42.clone, s32[256]{0:T(256)S(1)} %get-tuple-element.7, f32[256,64,128]{2,1,0:T(8,128)} %fusion.13), kind=kCustom, calls=%fused_computation.5 | custom fusion | flops 2097152 | bytes 25166848 | tf_op jit(solution)/shard_map/scatter-add | solution.py:50
  180.9 0.8 convert_element_type.39
  181.8 0.0 all-reduce.9.cloned.1.call-start
  181.8 32.2 %all-reduce.7.cloned.1.call-done = bf16[24,64,128]{2,1,0:T(8,128)(2,1)} async-done(((bf16[24,64,128]{2,1,0:T(8,128)(2,1)}), bf16[24,64,128]{2,1,0:T(8,128)(2,1)}) %all-reduce.7.cloned.1.call-update) | async-done | bytes 393232 | tf_op jit(solution)/shard_map/psum | solution.py:53
  214.1 1.2 fusion.4
  215.2 21.5 %psum.59 = f32[64]{0:T(128)S(1)} all-reduce(f32[64]{0:T(128)S(1)} %fusion.4), channel_id=1, replica_groups=mesh['row'=8,'col'=4] {'row'}, use_global_device_ids=true, to_apply=%region_8.9 | all-reduce | flops 64 | bytes 512 | tf_op jit(solution)/shard_map/psum | solution.py:54
  236.8 1.2 fusion.5
  238.0 3.1 gather_fusion.2
  241.0 10.2 %fusion.14 = f32[256,64,128]{2,1,0:T(8,128)} fusion(bf16[256,64,128]{2,1,0:T(8,128)(2,1)} %gather_fusion.2, bf16[256,128,128]{2,1,0:T(8,128)(2,1)} %param.7), kind=kOutput, calls=%fused_computation.52 | convolution fusion | flops 536870912 | bytes 20971520 | tf_op jit(solution)/shard_map/tkr,trc->tkc/dot_general | solution.py:37
  251.2 0.1 broadcast.40
  251.4 26.3 %scatter_fusion.2 = f32[32,64,128]{2,1,0:T(8,128)S(1)} fusion(f32[32,64,128]{2,1,0:T(8,128)S(1)} %broadcast.40, s32[256]{0:T(256)S(1)} %get-tuple-element.3, f32[256,64,128]{2,1,0:T(8,128)} %fusion.14), kind=kCustom, calls=%fused_computation.6 | custom fusion | flops 2097152 | bytes 25166848 | tf_op jit(solution)/shard_map/scatter-add | solution.py:40
  277.7 0.9 convert_element_type.42
  278.6 0.0 all-reduce.9.cloned.1.call-update
  278.6 0.0 all-reduce.11.cloned.1.call-start
  278.6 69.0 %all-reduce.9.cloned.1.call-done = bf16[32,64,128]{2,1,0:T(8,128)(2,1)} async-done(((bf16[32,64,128]{2,1,0:T(8,128)(2,1)}), bf16[32,64,128]{2,1,0:T(8,128)(2,1)}) %all-reduce.9.cloned.1.call-update) | async-done | bytes 524304 | tf_op jit(solution)/shard_map/psum | solution.py:41
  347.7 1.3 fusion.2
  348.9 5.7 %psum.61 = f32[64]{0:T(128)S(1)} all-reduce(f32[64]{0:T(128)S(1)} %fusion.2), channel_id=1, replica_groups=mesh['row'=8,'col'=4] {'col'}, use_global_device_ids=true, to_apply=%region_12.13 | all-reduce | flops 64 | bytes 512 | tf_op jit(solution)/shard_map/psum | solution.py:42
  354.6 1.3 fusion.3
  355.9 3.1 gather_fusion.3
  358.9 13.7 %fusion.15 = f32[256,64,128]{2,1,0:T(8,128)} fusion(bf16[256,64,128]{2,1,0:T(8,128)(2,1)} %gather_fusion.3, bf16[256,128,128]{2,1,0:T(8,128)(2,1)} %param.7), kind=kOutput, calls=%fused_computation.53 | convolution fusion | flops 536870912 | bytes 20971520 | tf_op jit(solution)/shard_map/tkc,trc->tkr/dot_general | solution.py:47
  372.7 0.1 broadcast.42
  372.7 26.3 %scatter_fusion.3 = f32[24,64,128]{2,1,0:T(8,128)S(1)} fusion(f32[24,64,128]{2,1,0:T(8,128)S(1)} %broadcast.42, s32[256]{0:T(256)S(1)} %get-tuple-element.7, f32[256,64,128]{2,1,0:T(8,128)} %fusion.15), kind=kCustom, calls=%fused_computation.7 | custom fusion | flops 2097152 | bytes 25166848 | tf_op jit(solution)/shard_map/scatter-add | solution.py:50
  399.1 0.8 convert_element_type.45
  399.9 0.6 constant_dynamic-slice_fusion
  400.5 31.6 %all-reduce.11.cloned.1.call-done = bf16[24,64,128]{2,1,0:T(8,128)(2,1)} async-done(((bf16[24,64,128]{2,1,0:T(8,128)(2,1)}), bf16[24,64,128]{2,1,0:T(8,128)(2,1)}) %all-reduce.11.cloned.1.call-update) | async-done | bytes 393232 | tf_op jit(solution)/shard_map/psum | solution.py:53
  432.2 1.2 fusion.6
  433.4 21.4 %psum.63 = f32[64]{0:T(128)S(1)} all-reduce(f32[64]{0:T(128)S(1)} %fusion.6), channel_id=1, replica_groups=mesh['row'=8,'col'=4] {'row'}, use_global_device_ids=true, to_apply=%region_16.17 | all-reduce | flops 64 | bytes 512 | tf_op jit(solution)/shard_map/psum | solution.py:54
  454.7 1.9 fusion.7
  (8 shorter events, 0.1 us)
Async XLA Ops:
  7.2 122.4 %all-reduce.5.cloned.1.call-start = ((), (), s32[]{:S(2)}) async-start(), calls=%async_computation | async-start | bytes 1048576 | tf_op jit(solution)/shard_map/psum | solution.py:41
  54.2 159.9 %all-reduce.7.cloned.1.call-start = ((), (), s32[]{:S(2)}) async-start(), calls=%async_computation.1 | async-start | bytes 786432 | tf_op jit(solution)/shard_map/psum | solution.py:53
  181.8 165.9 %all-reduce.9.cloned.1.call-start = ((), (), s32[]{:S(2)}) async-start(), calls=%async_computation.2 | async-start | bytes 1048576 | tf_op jit(solution)/shard_map/psum | solution.py:41
  278.6 153.6 %all-reduce.11.cloned.1.call-start = ((), (), s32[]{:S(2)}) async-start(), calls=%async_computation.3 | async-start | bytes 786432 | tf_op jit(solution)/shard_map/psum | solution.py:53
Sparse Core Ops, SparseCore 0:
  54.3 75.2 all-reduce.4
  181.9 32.1 all-reduce.6
  278.7 68.9 all-reduce.8
  400.0 32.1 all-reduce.10
where the time goes:
time: 467 us; the launch traced here: 463 us
  waiting for transfers between devices  208 us (45%)
  other arithmetic  124 us (27%)
  blocking collectives  54.2 us (12%)
  matrix products  47.9 us (10%)
  between operations  14.6 us (3%)
  local copies, waits for them, and re-layouts  14.5 us (3%)
    psum x2, waiting for transfers between devices, local(): lax.psum(set_terms.astype(jnp.bfloat16), 'row').astype(jnp.float32)  144 us
    psum x2, waiting for transfers between devices, local(): lax.psum(hub_terms.astype(jnp.bfloat16), 'col').astype(jnp.float32)  63.9 us
    scatter-add x2, other arithmetic, local(): jax.ops.segment_sum(back_products, row_slot, num_segments=slot_count, mod...  52.6 us
    scatter-add x2, other arithmetic, local(): jax.ops.segment_sum(products, col_slot, num_segments=set_blocks, mode='dr...  52.6 us
    psum x2, blocking collectives, local(): squares = lax.psum(jnp.sum(raw_hub * raw_hub, axis=(0, 2)), 'row')  42.9 us
    dot_general x2, matrix products, local(): jnp.einsum('tkc,trc->tkr', picked_cols, tile_blocks, preferred_element_ty...  27.5 us
    dot_general x2, matrix products, local(): jnp.einsum('tkr,trc->tkc', picked, tile_blocks, preferred_element_type=jn...  20.4 us
    psum x2, blocking collectives, local(): squares = lax.psum(jnp.sum(raw_set * raw_set, axis=(0, 2)), 'col')  11.3 us
  transfers between devices with their start and end apart: 4, of which 4 were waited for; matrix products, arithmetic and copies ran while one was open for 0% of the time, Pallas kernels for 0%

commit v1 on v0

--- a/solution.py
+++ b/solution.py
@@ -5,6 +5,11 @@
 
 ITERS = 2
 RB_DEV = 16
+
+
+def summed_here(block, name):
+    blocks = lax.all_gather(block, name)
+    return jnp.sum(blocks, axis=0)
 
 
 def local(hub_seeds, tile_blocks, tile_rows, tile_cols, tile_count, row_blocks):
@@ -38,7 +43,7 @@
             "tkr,trc->tkc", picked, tile_blocks, preferred_element_type=jnp.float32
         )
         set_terms = jax.ops.segment_sum(products, col_slot, num_segments=set_blocks, mode="drop")
-        raw_set = lax.psum(set_terms.astype(jnp.bfloat16), "row").astype(jnp.float32)
+        raw_set = summed_here(set_terms.astype(jnp.bfloat16), "row").astype(jnp.float32)
         squares = lax.psum(jnp.sum(raw_set * raw_set, axis=(0, 2)), "col")
         factor = 1.0 / jnp.sqrt(squares / host_count + 1.0)
         column_set = (raw_set * factor[None, :, None]).astype(jnp.bfloat16)

time: 467 us -> 468 us (level)
    all_gather x0 -> x2, waiting for transfers between devices: none -> 145 us  [summed_here(): blocks = lax.all_gather(block, name)]
    psum x2 -> x0, waiting for transfers between devices: 144 us -> none  [local(): lax.psum(set_terms.astype(jnp.bfloat16), 'row').astype(jnp.float32)]
    reduce_sum x0 -> x2, other arithmetic: none -> 6.19 us  [summed_here(): return jnp.sum(blocks, axis=0)]
where the time goes in v1:
time: 468 us; the launch traced here: 464 us
  waiting for transfers between devices  207 us (44%)
  other arithmetic  126 us (27%)
  blocking collectives  54.2 us (12%)
  matrix products  47.9 us (10%)
  between operations  14.6 us (3%)
  local copies, waits for them, and re-layouts  14.5 us (3%)
    all_gather x2, waiting for transfers between devices, summed_here(): blocks = lax.all_gather(block, name)  145 us
    psum x2, waiting for transfers between devices, local(): lax.psum(hub_terms.astype(jnp.bfloat16), 'col').astype(jnp.float32)  62.6 us
    scatter-add x2, other arithmetic, local(): jax.ops.segment_sum(back_products, row_slot, num_segments=slot_count, mod...  52.6 us
    scatter-add x2, other arithmetic, local(): jax.ops.segment_sum(products, col_slot, num_segments=set_blocks, mode='dr...  52.6 us
    psum x2, blocking collectives, local(): squares = lax.psum(jnp.sum(raw_hub * raw_hub, axis=(0, 2)), 'row')  42.9 us
    dot_general x2, matrix products, local(): jnp.einsum('tkc,trc->tkr', picked_cols, tile_blocks, preferred_element_ty...  27.5 us
    dot_general x2, matrix products, local(): jnp.einsum('tkr,trc->tkc', picked, tile_blocks, preferred_element_type=jn...  20.4 us
    psum x2, blocking collectives, local(): squares = lax.psum(jnp.sum(raw_set * raw_set, axis=(0, 2)), 'col')  11.3 us
  transfers between devices with their start and end apart: 4, of which 4 were waited for; matrix products, arithmetic and copies ran while one was open for 0% of the time, Pallas kernels for 0%

profile of v1, /device:TPU:0, one launch (start us, length us, event | category | flops | bytes accessed | tf_op | source)
XLA Modules:
  0.0 464.2 jit_solution(10246737490859987426)
XLA Ops:
  7.2 0.0 all-gather.5.cloned.1.call-start
  7.2 1.3 fusion.10
  8.5 1.2 dynamic_slice.6
  9.7 0.6 iota_compare_fusion.1
  11.0 1.4 broadcast_clamp_fusion
  12.4 1.1 broadcast_select_fusion
  13.5 3.1 gather_fusion
  16.6 10.2 %fusion.12 = f32[256,64,128]{2,1,0:T(8,128)} fusion(bf16[256,64,128]{2,1,0:T(8,128)(2,1)} %gather_fusion, bf16[256,128,128]{2,1,0:T(8,128)(2,1)} %param.7), kind=kOutput, calls=%fused_computation.50 | convolution fusion | flops 536870912 | bytes 20971520 | tf_op jit(solution)/shard_map/tkr,trc->tkc/dot_general | solution.py:42
  26.8 0.1 broadcast.40.clone
  26.9 26.3 %scatter_fusion = f32[32,64,128]{2,1,0:T(8,128)S(1)} fusion(f32[32,64,128]{2,1,0:T(8,128)S(1)} %broadcast.40.clone, s32[256]{0:T(256)S(1)} %get-tuple-element.3, f32[256,64,128]{2,1,0:T(8,128)} %fusion.12), kind=kCustom, calls=%fused_computation.4 | custom fusion | flops 2097152 | bytes 25166848 | tf_op jit(solution)/shard_map/scatter-add | solution.py:45
  53.2 0.9 convert_element_type.40
  54.1 0.0 all-reduce.3.cloned.1.call-start
  54.2 75.5 %all-gather.5.cloned.1.call-done = bf16[256,64,128]{2,1,0:T(8,128)(2,1)} async-done(((bf16[32,64,128]{2,1,0:T(8,128)(2,1)}), bf16[256,64,128]{2,1,0:T(8,128)(2,1)}) %all-gather.5.cloned.1.call-update) | async-done | bytes 4194320 | tf_op jit(solution)/shard_map/all_gather | solution.py:11
  129.7 3.1 reduce_sum.70
  132.8 0.2 fusion
  133.0 5.7 %psum.42 = f32[64]{0:T(128)S(1)} all-reduce(f32[64]{0:T(128)S(1)} %fusion), channel_id=1, replica_groups=mesh['row'=8,'col'=4] {'col'}, use_global_device_ids=true, to_apply=%region_4.5 | all-reduce | flops 64 | bytes 512 | tf_op jit(solution)/shard_map/psum | solution.py:47
  138.7 0.2 fusion.1
  138.9 3.1 gather_fusion.1
  142.0 13.7 %fusion.13 = f32[256,64,128]{2,1,0:T(8,128)} fusion(bf16[256,64,128]{2,1,0:T(8,128)(2,1)} %gather_fusion.1, bf16[256,128,128]{2,1,0:T(8,128)(2,1)} %param.7), kind=kOutput, calls=%fused_computation.51 | convolution fusion | flops 536870912 | bytes 20971520 | tf_op jit(solution)/shard_map/tkc,trc->tkr/dot_general | solution.py:52
  155.7 0.1 broadcast.42.clone
  155.8 26.3 %scatter_fusion.1 = f32[24,64,128]{2,1,0:T(8,128)S(1)} fusion(f32[24,64,128]{2,1,0:T(8,128)S(1)} %broadcast.42.clone, s32[256]{0:T(256)S(1)} %get-tuple-element.7, f32[256,64,128]{2,1,0:T(8,128)} %fusion.13), kind=kCustom, calls=%fused_computation.5 | custom fusion | flops 2097152 | bytes 25166848 | tf_op jit(solution)/shard_map/scatter-add | solution.py:55
  182.1 0.8 convert_element_type.43
  182.9 0.0 all-gather.7.cloned.1.call-start
  183.0 31.6 %all-reduce.3.cloned.1.call-done = bf16[24,64,128]{2,1,0:T(8,128)(2,1)} async-done(((bf16[24,64,128]{2,1,0:T(8,128)(2,1)}), bf16[24,64,128]{2,1,0:T(8,128)(2,1)}) %all-reduce.3.cloned.1.call-update) | async-done | bytes 393232 | tf_op jit(solution)/shard_map/psum | solution.py:58
  214.6 1.2 fusion.4
  215.8 21.5 %psum.44 = f32[64]{0:T(128)S(1)} all-reduce(f32[64]{0:T(128)S(1)} %fusion.4), channel_id=1, replica_groups=mesh['row'=8,'col'=4] {'row'}, use_global_device_ids=true, to_apply=%region_8.9 | all-reduce | flops 64 | bytes 512 | tf_op jit(solution)/shard_map/psum | solution.py:59
  237.3 1.2 fusion.5
  238.5 3.1 gather_fusion.2
  241.6 10.2 %fusion.14 = f32[256,64,128]{2,1,0:T(8,128)} fusion(bf16[256,64,128]{2,1,0:T(8,128)(2,1)} %gather_fusion.2, bf16[256,128,128]{2,1,0:T(8,128)(2,1)} %param.7), kind=kOutput, calls=%fused_computation.52 | convolution fusion | flops 536870912 | bytes 20971520 | tf_op jit(solution)/shard_map/tkr,trc->tkc/dot_general | solution.py:42
  251.8 0.1 broadcast.40
  251.9 26.3 %scatter_fusion.2 = f32[32,64,128]{2,1,0:T(8,128)S(1)} fusion(f32[32,64,128]{2,1,0:T(8,128)S(1)} %broadcast.40, s32[256]{0:T(256)S(1)} %get-tuple-element.3, f32[256,64,128]{2,1,0:T(8,128)} %fusion.14), kind=kCustom, calls=%fused_computation.6 | custom fusion | flops 2097152 | bytes 25166848 | tf_op jit(solution)/shard_map/scatter-add | solution.py:45
  278.2 0.9 convert_element_type.46
  279.1 0.0 all-reduce.5.cloned.1.call-start
  279.1 69.2 %all-gather.7.cloned.1.call-done = bf16[256,64,128]{2,1,0:T(8,128)(2,1)} async-done(((bf16[32,64,128]{2,1,0:T(8,128)(2,1)}), bf16[256,64,128]{2,1,0:T(8,128)(2,1)}) %all-gather.7.cloned.1.call-update) | async-done | bytes 4194320 | tf_op jit(solution)/shard_map/all_gather | solution.py:11
  348.3 3.1 reduce_sum.73
  351.4 0.2 fusion.2
  351.6 5.7 %psum.45 = f32[64]{0:T(128)S(1)} all-reduce(f32[64]{0:T(128)S(1)} %fusion.2), channel_id=1, replica_groups=mesh['row'=8,'col'=4] {'col'}, use_global_device_ids=true, to_apply=%region_12.13 | all-reduce | flops 64 | bytes 512 | tf_op jit(solution)/shard_map/psum | solution.py:47
  357.3 0.2 fusion.3
  357.5 3.1 gather_fusion.3
  360.6 13.7 %fusion.15 = f32[256,64,128]{2,1,0:T(8,128)} fusion(bf16[256,64,128]{2,1,0:T(8,128)(2,1)} %gather_fusion.3, bf16[256,128,128]{2,1,0:T(8,128)(2,1)} %param.7), kind=kOutput, calls=%fused_computation.53 | convolution fusion | flops 536870912 | bytes 20971520 | tf_op jit(solution)/shard_map/tkc,trc->tkr/dot_general | solution.py:52
  374.3 0.1 broadcast.42
  374.4 26.3 %scatter_fusion.3 = f32[24,64,128]{2,1,0:T(8,128)S(1)} fusion(f32[24,64,128]{2,1,0:T(8,128)S(1)} %broadcast.42, s32[256]{0:T(256)S(1)} %get-tuple-element.7, f32[256,64,128]{2,1,0:T(8,128)} %fusion.15), kind=kCustom, calls=%fused_computation.7 | custom fusion | flops 2097152 | bytes 25166848 | tf_op jit(solution)/shard_map/scatter-add | solution.py:55
  400.7 0.8 convert_element_type.49
  401.5 0.6 constant_dynamic-slice_fusion
  402.2 31.0 %all-reduce.5.cloned.1.call-done = bf16[24,64,128]{2,1,0:T(8,128)(2,1)} async-done(((bf16[24,64,128]{2,1,0:T(8,128)(2,1)}), bf16[24,64,128]{2,1,0:T(8,128)(2,1)}) %all-reduce.5.cloned.1.call-update) | async-done | bytes 393232 | tf_op jit(solution)/shard_map/psum | solution.py:58
  433.2 1.2 fusion.6
  434.4 21.4 %psum.47 = f32[64]{0:T(128)S(1)} all-reduce(f32[64]{0:T(128)S(1)} %fusion.6), channel_id=1, replica_groups=mesh['row'=8,'col'=4] {'row'}, use_global_device_ids=true, to_apply=%region_16.17 | all-reduce | flops 64 | bytes 512 | tf_op jit(solution)/shard_map/psum | solution.py:59
  455.7 1.9 fusion.7
  (10 shorter events, 0.1 us)
Async XLA Ops:
  7.2 122.5 %all-gather.5.cloned.1.call-start = ((), (), s32[]{:S(2)}) async-start(), calls=%async_computation.2 | async-start | bytes 4718592 | tf_op jit(solution)/shard_map/all_gather | solution.py:11
  54.1 160.4 %all-reduce.3.cloned.1.call-start = ((), (), s32[]{:S(2)}) async-start(), calls=%async_computation | async-start | bytes 786432 | tf_op jit(solution)/shard_map/psum | solution.py:58
  182.9 165.4 %all-gather.7.cloned.1.call-start = ((), (), s32[]{:S(2)}) async-start(), calls=%async_computation.3 | async-start | bytes 4718592 | tf_op jit(solution)/shard_map/all_gather | solution.py:11
  279.1 154.1 %all-reduce.5.cloned.1.call-start = ((), (), s32[]{:S(2)}) async-start(), calls=%async_computation.1 | async-start | bytes 786432 | tf_op jit(solution)/shard_map/psum | solution.py:58
Sparse Core Ops, SparseCore 0:
  54.3 75.3 all-gather.4
  183.1 31.4 all-reduce.2
  279.2 69.0 all-gather.6
  401.7 31.4 all-reduce.4
